TPU v7x, 256 devices: a 2x2x32 block of a 4x8x32 slice. The times are simulated.
256 devices in a mesh: cuts: 4 (over y, x), wide: 32 (over z), batch: 2 (over core).
Axes of the slice: x: 2, y: 2, z: 32, core: 2. Of those that a mesh axis runs over, the one named last changes fastest.
The devices are a block of a 4x8x32 slice.
Arguments:
- initial: bfloat16 [2, 128, 2, 2, 256, 256], P('batch', 'cuts', None, None, None, 'wide'), parts along dimension 1, may hold values from -6 to 6
- branches: bfloat16 [8, 2, 2, 256, 2, 256], P(None, None, None, 'batch'), may hold values from -0.1875 to 0.1875
- projectors: float32 [8, 2, 2, 2], replicated, may hold values from -4 to 4
- bits: int32 [2, 8], P('batch'), may hold values from 0 to 1
Outputs:
- amplitudes: float32 [2, 128, 2, 2, 256, 256], P('batch', 'cuts', None, None, 'wide'), parts along dimension 1
There are 4 independent parts, one for each index of `cuts`. A program takes and returns all parts, laid end to end along the dimension named above; an argument that names none is the same for every part. Nothing has to cross between parts.
Inputs may be any that keep to these rules, and one draw needn't show every extreme that they name: `bits`: each entry is a bit.
All inputs are finite; a program needn't handle non-finite values.
Results may differ from a plain program's by a relative error of at most 0.014.
Values may be sent and summed in bfloat16 or wider, within the bound.
No kernel may reach another device: no remote copies, remote signals or barrier semaphores. Data moves between devices by JAX's collectives and lax.ppermute only.
A program may use at most 64 MiB of HBM per device.

v0:
```python
import jax
import jax.numpy as jnp
from jax import lax
from jax.sharding import PartitionSpec as P


def copy_for_each(value, axis):
    copies = jnp.broadcast_to(value, (lax.axis_size(axis), *value.shape))
    return lax.all_to_all(copies, axis, split_axis=0, concat_axis=0, tiled=True)


def laid_out(pieces, dim):
    pieces = jnp.moveaxis(pieces, 0, dim)
    lengths = pieces.shape
    return pieces.reshape(*lengths[:dim], lengths[dim] * lengths[dim + 1], *lengths[dim + 2 :])


def gathered_copies(value, axis, dim):
    pieces = copy_for_each(value, axis)
    return laid_out(pieces, dim)


def contract(state, branch, select):
    prod = jnp.einsum("ncphuv,thugw->ncptgvw", state, branch, preferred_element_type=jnp.float32)
    real_part = prod[:, :, 0, 0] - prod[:, :, 1, 1]
    imag_part = prod[:, :, 0, 1] + prod[:, :, 1, 0]
    proj_re = select[:, 0][:, None, :, None, None]
    proj_im = select[:, 1][:, None, :, None, None]
    out_re = proj_re * real_part - proj_im * imag_part
    out_im = proj_re * imag_part + proj_im * real_part
    return jnp.stack([out_re, out_im], axis=2)


def advance(block, branch, select, final):
    result = contract(block, branch, select)
    if final:
        return result
    return result.astype(jnp.bfloat16)


def branch_of(branches, step):
    return gathered_copies(branches[step], "batch", 2)


def select_of(projectors, bits, step):
    chosen = (bits[:, step] == 1)[:, None, None]
    return jnp.where(chosen, projectors[step, 1][None], projectors[step, 0][None])


def shards(initial, branches, projectors, bits):
    steps_total = branches.shape[0]
    state = lax.all_to_all(initial, "wide", split_axis=1, concat_axis=5, tiled=True)
    for step in range(steps_total):
        branch = branch_of(branches, step)
        select = select_of(projectors, bits, step)
        state = advance(state, branch, select, step == steps_total - 1)
    return lax.all_to_all(state, "wide", split_axis=4, concat_axis=1, tiled=True)


def solution(mesh):
    in_specs = (
        P("batch", "cuts", None, None, None, "wide"),
        P(None, None, None, "batch", None, None),
        P(),
        P("batch", None),
    )
    out_specs = P("batch", "cuts", None, None, "wide", None)
    return jax.shard_map(shards, mesh=mesh, in_specs=in_specs, out_specs=out_specs, check_vma=False)
```

profile of v0, /device:TPU:37, one launch (start us, length us, event | category | flops | bytes accessed | tf_op | source)
XLA Modules:
  0.0 275.5 jit_solution(9295105258477170813)
XLA Ops:
  0.0 6.0 %slice_bitcast_fusion.9 = (bf16[2,2,128,2,256]{4,3,2,1,0:T(2,128)(2,1)S(1)}, bf16[2,2,128,2,256]{4,3,2,1,0:T(2,128)(2,1)}, bf16[2,2,128,2,256]{4,3,2,1,0:T(2,128...) fusion(bf16[8,2,2,128,2,256]{5,4,3,2,1,0:T(2,128)(2,1)} %param.5), kind=kLoop, calls=%fused_computation.91 | loop fusion | bytes 8388608 | tf_op jit(solution)/shard_map/squeeze | solution.py:42
  6.4 1.2 broadcast_in_dim.107
  7.6 24.0 %all-to-all-start = ((bf16[2,2,2,128,2,256]{3,5,2,4,1,0:T(8,128)(2,1)}), bf16[2,2,2,128,2,256]{3,5,2,4,1,0:T(8,128)(2,1)S(1)}, u32[]{:S(2)}, u32[]{:S(2)}) async-start(bf16[2,2,2,128,2,256]{3,5,2,4,1,0:T(8,128)(2,1)} %broadcast_in_dim.107), calls=%async_computation | async-start | bytes 2097152 | tf_op jit(solution)/shard_map/all_to_all | solution.py:9
  31.6 0.9 copy.49
  33.0 0.9 copy.57
  33.9 0.9 copy.60
  34.8 0.9 copy.63
  35.7 0.9 copy.66
  36.5 1.1 broadcast_in_dim.108
  37.7 5.1 %all_to_all.73 = bf16[2,2,2,128,2,256]{5,3,2,4,1,0:T(8,128)(2,1)} all-to-all(bf16[2,2,2,128,2,256]{5,3,2,4,1,0:T(8,128)(2,1)S(1)} %broadcast_in_dim.108), channel_id=1, replica_groups=mesh['cuts'=4,'wide'=32,'batch'=2] {'batch'}, dimensions={0} | all-to-all | bytes 2097152 | tf_op jit(solution)/shard_map/all_to_all | solution.py:9
  42.8 4.6 %all_to_all.74 = bf16[2,2,2,128,2,256]{5,3,2,4,1,0:T(8,128)(2,1)S(1)} all-to-all(bf16[2,2,2,128,2,256]{5,3,2,4,1,0:T(8,128)(2,1)S(1)} %broadcast_in_dim.109), channel_id=1, replica_groups=mesh['cuts'=4,'wide'=32,'batch'=2] {'batch'}, dimensions={0} | all-to-all | bytes 2097152 | tf_op jit(solution)/shard_map/all_to_all | solution.py:9
  47.5 4.7 %all_to_all.75 = bf16[2,2,2,128,2,256]{5,3,2,4,1,0:T(8,128)(2,1)S(1)} all-to-all(bf16[2,2,2,128,2,256]{5,3,2,4,1,0:T(8,128)(2,1)S(1)} %broadcast_in_dim.110), channel_id=1, replica_groups=mesh['cuts'=4,'wide'=32,'batch'=2] {'batch'}, dimensions={0} | all-to-all | bytes 2097152 | tf_op jit(solution)/shard_map/all_to_all | solution.py:9
  52.4 5.5 %all_to_all.76 = bf16[2,2,2,128,2,256]{5,3,2,4,1,0:T(8,128)(2,1)} all-to-all(bf16[2,2,2,128,2,256]{5,3,2,4,1,0:T(8,128)(2,1)S(1)} %broadcast_in_dim.111), channel_id=1, replica_groups=mesh['cuts'=4,'wide'=32,'batch'=2] {'batch'}, dimensions={0} | all-to-all | bytes 2097152 | tf_op jit(solution)/shard_map/all_to_all | solution.py:9
  58.0 5.5 %all_to_all.77 = bf16[2,2,2,128,2,256]{5,3,2,4,1,0:T(8,128)(2,1)} all-to-all(bf16[2,2,2,128,2,256]{5,3,2,4,1,0:T(8,128)(2,1)S(1)} %broadcast_in_dim.112), channel_id=1, replica_groups=mesh['cuts'=4,'wide'=32,'batch'=2] {'batch'}, dimensions={0} | all-to-all | bytes 2097152 | tf_op jit(solution)/shard_map/all_to_all | solution.py:9
  63.7 5.5 %all_to_all.78 = bf16[2,2,2,128,2,256]{5,3,2,4,1,0:T(8,128)(2,1)} all-to-all(bf16[2,2,2,128,2,256]{5,3,2,4,1,0:T(8,128)(2,1)S(1)} %broadcast_in_dim.113), channel_id=1, replica_groups=mesh['cuts'=4,'wide'=32,'batch'=2] {'batch'}, dimensions={0} | all-to-all | bytes 2097152 | tf_op jit(solution)/shard_map/all_to_all | solution.py:9
  69.3 5.4 %all_to_all.79 = bf16[2,2,2,128,2,256]{5,3,2,4,1,0:T(8,128)(2,1)} all-to-all(bf16[2,2,2,128,2,256]{5,3,2,4,1,0:T(8,128)(2,1)S(1)} %broadcast_in_dim.114), channel_id=1, replica_groups=mesh['cuts'=4,'wide'=32,'batch'=2] {'batch'}, dimensions={0} | all-to-all | bytes 2097152 | tf_op jit(solution)/shard_map/all_to_all | solution.py:9
  74.7 13.7 %all-to-all-start.1 = ((bf16[1,32,2,2,256,8]{4,5,3,2,0,1:T(8,128)(2,1)}), bf16[1,32,2,2,256,8]{4,5,3,2,0,1:T(8,128)(2,1)}, u32[]{:S(2)}, u32[]{:S(2)}) async-start(bf16[1,32,2,2,256,8]{4,5,3,2,0,1:T(8,128)(2,1)} %bitcast.356), calls=%async_computation.1 | async-start | bytes 1048576 | tf_op jit(solution)/shard_map/all_to_all | solution.py:52
  92.8 2.0 copy.43
  94.9 2.6 reshape.1163
  97.5 1.0 copy.50
  99.8 1.1 copy.52
  100.9 1.1 copy.55
  102.0 1.0 copy.58
  104.9 47.1 %all-to-all-done.1 = bf16[1,32,2,2,256,8]{4,5,3,2,0,1:T(8,128)(2,1)} async-done(((bf16[1,32,2,2,256,8]{4,5,3,2,0,1:T(8,128)(2,1)}), bf16[1,32,2,2,256,8]{4,5,3,2,0,1:T(8,128)(2,1)}, u32[]{:S(2)}, u32[]{:S(2)}) %all-to-all-start.1) | async-done | bytes 524320 | tf_op jit(solution)/shard_map/all_to_all | solution.py:52
  152.0 2.1 convolution_bitcast_fusion.7
  154.4 1.0 copy-done.3
  156.3 1.0 copy-done.2
  158.3 1.0 copy-done.1
  160.2 1.0 copy-done
  165.2 0.8 copy.69
  166.0 108.3 %all_to_all.80 = f32[1,1,2,2,256,256]{5,3,2,1,0,4:T(2,128)S(1)} all-to-all(f32[1,1,2,2,256,256]{5,3,2,1,0,4:T(2,128)S(1)} %copy.69), channel_id=1, replica_groups=mesh['cuts'=4,'wide'=32,'batch'=2] {'wide'}, dimensions={4} | all-to-all | bytes 2097152 | tf_op jit(solution)/shard_map/all_to_all | solution.py:57
  274.3 1.2 copy.108
  (72 shorter events, 11.1 us)
Async XLA Ops:
  7.6 28.9 %all-to-all-start = ((bf16[2,2,2,128,2,256]{3,5,2,4,1,0:T(8,128)(2,1)}), bf16[2,2,2,128,2,256]{3,5,2,4,1,0:T(8,128)(2,1)S(1)}, u32[]{:S(2)}, u32[]{:S(2)}) async-start(bf16[2,2,2,128,2,256]{3,5,2,4,1,0:T(8,128)(2,1)} %broadcast_in_dim.107), calls=%async_computation | async-start | bytes 2097152 | tf_op jit(solution)/shard_map/all_to_all | solution.py:9
  31.6 1.2 copy-start.15
  31.6 1.4 copy-start.14
  31.6 2.3 copy-start.13
  47.4 4.8 %copy-start.12 = (bf16[2,2,128,2,256]{4,2,1,3,0:T(8,128)(2,1)S(1)}, bf16[2,2,128,2,256]{4,2,1,3,0:T(8,128)(2,1)}, u32[]{:S(2)}) copy-start(bf16[2,2,128,2,256]{4,2,1,3,0:T(8,128)(2,1)} %copy.57) | copy-start | bytes 1572868
  52.3 5.6 %copy-start.11 = (bf16[2,2,128,2,256]{4,2,1,3,0:T(8,128)(2,1)S(1)}, bf16[2,2,128,2,256]{4,2,1,3,0:T(8,128)(2,1)}, u32[]{:S(2)}) copy-start(bf16[2,2,128,2,256]{4,2,1,3,0:T(8,128)(2,1)} %copy.60) | copy-start | bytes 1572868
  57.9 5.7 %copy-start.10 = (bf16[2,2,128,2,256]{4,2,1,3,0:T(8,128)(2,1)S(1)}, bf16[2,2,128,2,256]{4,2,1,3,0:T(8,128)(2,1)}, u32[]{:S(2)}) copy-start(bf16[2,2,128,2,256]{4,2,1,3,0:T(8,128)(2,1)} %copy.63) | copy-start | bytes 1572868
  63.6 5.6 %copy-start.9 = (bf16[2,2,128,2,256]{4,2,1,3,0:T(8,128)(2,1)S(1)}, bf16[2,2,128,2,256]{4,2,1,3,0:T(8,128)(2,1)}, u32[]{:S(2)}) copy-start(bf16[2,2,128,2,256]{4,2,1,3,0:T(8,128)(2,1)} %copy.66) | copy-start | bytes 1572868
  69.2 19.2 %copy-start.17 = (s32[1,8]{1,0:T(1,128)S(1)}, s32[1,8]{1,0:T(1,128)}, u32[]{:S(2)}) copy-start(s32[1,8]{1,0:T(1,128)} %param.7) | copy-start | bytes 100
  74.7 77.3 %all-to-all-start.1 = ((bf16[1,32,2,2,256,8]{4,5,3,2,0,1:T(8,128)(2,1)}), bf16[1,32,2,2,256,8]{4,5,3,2,0,1:T(8,128)(2,1)}, u32[]{:S(2)}, u32[]{:S(2)}) async-start(bf16[1,32,2,2,256,8]{4,5,3,2,0,1:T(8,128)(2,1)} %bitcast.356), calls=%async_computation.1 | async-start | bytes 1048576 | tf_op jit(solution)/shard_map/all_to_all | solution.py:52
  94.9 2.6 copy-start.4
  99.8 2.2 copy-start.5
  100.9 2.1 copy-start.6
  102.0 1.7 copy-start.7
  103.0 1.3 copy-start.8
  103.7 0.8 copy-start.16
  154.1 1.2 copy-start.3
  156.1 1.2 copy-start.2
  158.0 1.2 copy-start.1
  160.0 1.2 copy-start
where the time goes:
time: 281 us; the launch traced here: 275 us
  blocking collectives  145 us (52%)
  waiting for transfers between devices  47.1 us (17%)
  starting transfers between devices  37.7 us (13%)
  local copies, waits for them, and re-layouts  31.1 us (11%)
  matrix products  7.15 us (3%)
  between operations  5.39 us (2%)
    all_to_all x1, blocking collectives, shards(): lax.all_to_all(state, 'wide', split_axis=4, concat_axis=1, tiled=True)  108 us
    all_to_all x1, waiting for transfers between devices, shards(): lax.all_to_all(initial, 'wide', split_axis=1, concat_axis=5, tiled=True)  47.1 us
    all_to_all x7, blocking collectives, copy_for_each(): return lax.all_to_all(copies, axis, split_axis=0, concat_axis=0, tiled=True)  36.3 us
    all_to_all x1, starting transfers between devices, copy_for_each(): return lax.all_to_all(copies, axis, split_axis=0, concat_axis=0, tiled=True)  24 us
    all_to_all x1, starting transfers between devices, shards(): lax.all_to_all(initial, 'wide', split_axis=1, concat_axis=5, tiled=True)  13.7 us
    squeeze x9, local copies, waits for them, and re-layouts, branch_of(): return gathered_copies(branches[step], 'batch', 2)  11 us
    dot_general x8, matrix products, contract(): jnp.einsum('ncphuv,thugw->ncptgvw', state, branch, preferred_element_type...  7.15 us
    transpose x8, local copies, waits for them, and re-layouts, laid_out(): pieces = jnp.moveaxis(pieces, 0, dim)  6.56 us
  transfers between devices with their start and end apart: 2, of which 1 were waited for; matrix products, arithmetic and copies ran while one was open for 5% of the time, Pallas kernels for 0%

commit v1 on v0

v1 whole, which is shorter than its diff:
```python
import functools

import jax
import jax.numpy as jnp
from jax import lax
from jax.experimental import pallas as pl
from jax.experimental.pallas import tpu as pltpu
from jax.sharding import PartitionSpec as P


def factor(proj_ref, bits_ref, step, g):
    bit = jnp.where(bits_ref[0, step] == 1, 1, 0)
    return proj_ref[step, bit, 0, g], proj_ref[step, bit, 1, g]


def project(real, imag, scale):
    scale_re, scale_im = scale
    return scale_re * real - scale_im * imag, scale_re * imag + scale_im * real


def weight_copies(w_ref, x_ref, buf, sem, transposed):
    me = lax.axis_index("batch")
    half = w_ref.shape[-1] if transposed else w_ref.shape[-2]
    copies = []
    for ref, owner in ((w_ref, me), (x_ref, 1 - me)):
        start = pl.multiple_of(owner * half, half)
        if transposed:
            blocks = ref.shape[1]
            for b in range(blocks):
                at = pl.multiple_of(owner * half + b * 2 * half, half)
                copies.append(pltpu.make_async_copy(ref.at[:, b], buf.at[:, :, pl.ds(at, half)], sem))
        else:
            copies.append(pltpu.make_async_copy(ref, buf.at[:, :, pl.ds(start, half), :], sem))
    return copies


def by_rows(got_ref, form):
    n, blocks, rows, q = got_ref.shape
    h = blocks // 2
    for k in range(blocks):
        block = got_ref[:, k].reshape(n * rows, q)
        if k < h:
            form[:, pl.ds((h + k) * q, q)] = block
        else:
            form[:, pl.ds((k - h) * q, q)] = block
            form[:, pl.ds((h + k) * q, q)] = -block


NN = (((1,), (0,)), ((), ()))
NT = (((1,), (1,)), ((), ()))


def dot(a, b, dims):
    return lax.dot_general(a, b, dims, preferred_element_type=jnp.float32)


def chain_kernel(n_steps, q, hs, proj_ref, bits_ref, got_ref, *refs):
    mine, other = refs[:n_steps], refs[n_steps : 2 * n_steps]
    out_ref = refs[2 * n_steps]
    bufs = refs[2 * n_steps + 1 : 3 * n_steps + 1]
    rows_form, cols_form, sems = refs[3 * n_steps + 1 :]
    last = n_steps - 1
    kinds = [s % 2 == 1 or s == last for s in range(n_steps)]
    copies = [weight_copies(mine[s], other[s], bufs[s], sems.at[s], kinds[s]) for s in range(n_steps)]
    for step in copies:
        for copy in step:
            copy.start()
    by_rows(got_ref, rows_form)
    k = 2 * hs * q
    for s in range(n_steps):
        for copy in copies[s]:
            copy.wait()
        for g in range(hs):
            scale = factor(proj_ref, bits_ref, s, g)
            if s == last:
                w = bufs[s][g]
                real = dot(w, rows_form[:, pl.ds(hs * q, k)], NT)
                imag = dot(w, rows_form[:, pl.ds(0, k)], NT)
                real, imag = project(real, imag, scale)
                n, _, part, _ = out_ref.shape
                out_ref[:, g] = real.astype(out_ref.dtype).reshape(n, part, q)
                out_ref[:, hs + g] = imag.astype(out_ref.dtype).reshape(n, part, q)
            elif s % 2 == 0:
                w = bufs[s][g].reshape(k, q)
                real = dot(rows_form[:, pl.ds(hs * q, k)], w, NN)
                imag = dot(rows_form[:, pl.ds(0, k)], w, NN)
                real, imag = project(real, imag, scale)
                imag = imag.astype(cols_form.dtype)
                cols_form[pl.ds((hs + g) * q, q), :] = real.astype(cols_form.dtype)
                cols_form[pl.ds(g * q, q), :] = imag
                cols_form[pl.ds((2 * hs + g) * q, q), :] = -imag
            else:
                w = bufs[s][g]
                real = dot(w, cols_form[pl.ds(hs * q, k), :], NN)
                imag = dot(w, cols_form[pl.ds(0, k), :], NN)
                real, imag = project(real, imag, scale)
                imag = imag.astype(rows_form.dtype)
                rows_form[:, pl.ds((hs + g) * q, q)] = real.astype(rows_form.dtype)
                rows_form[:, pl.ds(g * q, q)] = imag
                rows_form[:, pl.ds((2 * hs + g) * q, q)] = -imag


def last_kernel(step, q, hs, proj_ref, bits_ref, got_ref, mine, other, out_ref, buf, rows_form, sem):
    copies = weight_copies(mine, other, buf, sem, False)
    for copy in copies:
        copy.start()
    by_rows(got_ref, rows_form)
    for copy in copies:
        copy.wait()
    k = 2 * hs * q
    n, _, _, part, _ = out_ref.shape
    for g in range(hs):
        w = buf[g].reshape(k, q)
        real = dot(rows_form[:, pl.ds(hs * q, k)], w, NN)
        imag = dot(rows_form[:, pl.ds(0, k)], w, NN)
        real, imag = project(real, imag, factor(proj_ref, bits_ref, step, g))
        out_ref[:, 0, g] = real.reshape(n, part, q)
        out_ref[:, 1, g] = imag.reshape(n, part, q)


SMEM = pl.BlockSpec(memory_space=pltpu.SMEM)
VMEM = pl.BlockSpec(memory_space=pltpu.VMEM)
ANY = pl.BlockSpec(memory_space=pl.ANY)


def laid_out(branches, step, transposed):
    b = branches[step]
    parts, hs, half, gs, q = b.shape
    if transposed:
        return b.transpose(3, 0, 1, 4, 2).reshape(gs, parts * hs, q, half)
    return b.transpose(3, 0, 1, 2, 4).reshape(gs, parts * hs, half, q)


def shards(initial, branches, projectors, bits):
    steps, parts, hs, half, _, q = branches.shape
    _, cols, _, _, _, part = initial.shape
    n_chain = steps - 1
    sent = jnp.swapaxes(initial, 4, 5).reshape(cols, parts * hs, part, q)
    swapped = lax.ppermute(branches, "batch", [(0, 1), (1, 0)])
    got = lax.all_to_all(sent, "wide", split_axis=0, concat_axis=0, tiled=True)
    kinds = [s % 2 == 1 or s == n_chain - 1 for s in range(n_chain)] + [False]
    mine = [laid_out(branches, s, kinds[s]) for s in range(steps)]
    other = [laid_out(swapped, s, kinds[s]) for s in range(steps)]
    bufs = [pltpu.VMEM((hs, q, parts * hs * q) if t else (hs, parts * hs, q, q), jnp.bfloat16) for t in kinds]
    flops = 2 * 2 * parts * hs * q * hs * q * q
    state = pl.pallas_call(
        functools.partial(chain_kernel, n_chain, q, hs),
        out_shape=jax.ShapeDtypeStruct((cols, parts * hs, part, q), jnp.bfloat16),
        in_specs=[SMEM, SMEM, VMEM] + [ANY] * (2 * n_chain),
        out_specs=VMEM,
        scratch_shapes=bufs[:n_chain]
        + [
            pltpu.VMEM((q, 3 * hs * q), jnp.bfloat16),
            pltpu.VMEM((3 * hs * q, q), jnp.bfloat16),
            pltpu.SemaphoreType.DMA((n_chain,)),
        ],
        compiler_params=pltpu.CompilerParams(vmem_limit_bytes=40 * 2**20),
        cost_estimate=pl.CostEstimate(flops=n_chain * flops, bytes_accessed=8 * 2**20, transcendentals=0),
        name="chain",
    )(projectors, bits, got, *mine[:n_chain], *other[:n_chain])
    back = lax.all_to_all(state, "wide", split_axis=0, concat_axis=0, tiled=True)
    out = pl.pallas_call(
        functools.partial(last_kernel, n_chain, q, hs),
        out_shape=jax.ShapeDtypeStruct((cols, parts, hs, part, q), jnp.float32),
        in_specs=[SMEM, SMEM, VMEM, ANY, ANY],
        out_specs=VMEM,
        scratch_shapes=[bufs[n_chain], pltpu.VMEM((q, 3 * hs * q), jnp.bfloat16), pltpu.SemaphoreType.DMA],
        compiler_params=pltpu.CompilerParams(vmem_limit_bytes=40 * 2**20),
        cost_estimate=pl.CostEstimate(flops=flops, bytes_accessed=3 * 2**20, transcendentals=0),
        name="last",
    )(projectors, bits, back, mine[n_chain], other[n_chain])
    return out[None]


def solution(mesh):
    in_specs = (
        P("batch", "cuts", None, None, None, "wide"),
        P(None, None, None, "batch", None, None),
        P(),
        P("batch", None),
    )
    out_specs = P("batch", "cuts", None, None, "wide", None)
    return jax.shard_map(shards, mesh=mesh, in_specs=in_specs, out_specs=out_specs, check_vma=False)
```

time: 281 us -> 189 us (0.67); the launches traced: 275 us -> 187 us
  blocking collectives: 145 us -> 0 us
  waiting for transfers between devices: 47.1 us -> 95.8 us
  local copies, waits for them, and re-layouts: 31.1 us -> 42.3 us
  Pallas kernels: 0 us -> 10 us
  matrix products: 7.15 us -> 0 us
  between operations: 5.39 us -> 0.12 us
    all_to_all x8 -> x0, blocking collectives: 145 us -> none  [the longest x1 108 us: shards(): lax.all_to_all(state, 'wide', split_axis=4, concat_axis=1, tiled=True)]
    all_to_all x2, waiting for transfers between devices: 47.1 us -> 95.8 us  [the longest x1 61.1 us: shards(): lax.all_to_all(state, 'wide', split_axis=0, concat_axis=0, tiled=True)]
    transpose x8 -> x18, local copies, waits for them, and re-layouts: 6.56 us -> 32.1 us  [the longest x10 19.8 us: laid_out(): return b.transpose(3, 0, 1, 2, 4).reshape(gs, parts * hs, half, q)]
    ppermute x0 -> x1, starting transfers between devices: none -> 20.4 us  [shards(): swapped = lax.ppermute(branches, 'batch', [(0, 1), (1, 0)])]
    all_to_all x2, starting transfers between devices: 37.7 us -> 18.3 us  [the longest x1 13.5 us: shards(): got = lax.all_to_all(sent, 'wide', split_axis=0, concat_axis=0, tiled=True)]
    squeeze x9 -> x0, local copies, waits for them, and re-layouts: 11 us -> none  [branch_of(): return gathered_copies(branches[step], 'batch', 2)]
    pallas_call x0 -> x2, Pallas kernels: none -> 10 us  [the longest x1 7.43 us: shards(): pl.pallas_call(functools.partial(chain_kernel, n_chain, q, hs), out_shape...]
    dot_general x8 -> x0, matrix products: 7.15 us -> none  [contract(): jnp.einsum('ncphuv,thugw->ncptgvw', state, branch, preferred_element_type...]
  transfers between devices with their start and end apart: 2 -> 3, of which waited for: 1 -> 2; matrix products, arithmetic and copies ran while one was open for 5% -> 17% of each run, Pallas kernels for 0% -> 0%
where the time goes in v1:
time: 189 us; the launch traced here: 187 us
  waiting for transfers between devices  95.8 us (51%)
  local copies, waits for them, and re-layouts  42.3 us (22%)
  starting transfers between devices  38.7 us (20%)
  Pallas kernels  10 us (5%)
    all_to_all x1, waiting for transfers between devices, shards(): lax.all_to_all(state, 'wide', split_axis=0, concat_axis=0, tiled=True)  61.1 us
    all_to_all x1, waiting for transfers between devices, shards(): got = lax.all_to_all(sent, 'wide', split_axis=0, concat_axis=0, tiled=True)  34.6 us
    ppermute x1, starting transfers between devices, shards(): swapped = lax.ppermute(branches, 'batch', [(0, 1), (1, 0)])  20.4 us
    transpose x10, local copies, waits for them, and re-layouts, laid_out(): return b.transpose(3, 0, 1, 2, 4).reshape(gs, parts * hs, half, q)  19.8 us
    all_to_all x1, starting transfers between devices, shards(): got = lax.all_to_all(sent, 'wide', split_axis=0, concat_axis=0, tiled=True)  13.5 us
    transpose x8, local copies, waits for them, and re-layouts, laid_out(): return b.transpose(3, 0, 1, 4, 2).reshape(gs, parts * hs, q, half)  12.3 us
    unnamed x25, local copies, waits for them, and re-layouts  10.3 us
    pallas_call x1, Pallas kernels, shards(): pl.pallas_call(functools.partial(chain_kernel, n_chain, q, hs), out_shape...  7.43 us
  transfers between devices with their start and end apart: 3, of which 2 were waited for; matrix products, arithmetic and copies ran while one was open for 17% of the time, Pallas kernels for 0%

profile of v1, /device:TPU:37, one launch (start us, length us, event | category | flops | bytes accessed | tf_op | source)
XLA Modules:
  0.0 187.0 jit_solution(10784432423003777480)
XLA Ops:
  0.0 20.4 %collective-permute-start = (bf16[8,2,2,128,2,256]{5,4,3,2,1,0:T(2,128)(2,1)}, bf16[8,2,2,128,2,256]{5,4,3,2,1,0:T(2,128)(2,1)}, u32[]{:S(2)}, u32[]{:S(2)}) collective-permute-start(bf16[8,2,2,128,2,256]{5,4,3,2,1,0:T(2,128)(2,1)} %param.5), channel_id=1, source_target_pairs={{0,1},{1,0},{2,3},{3,2},{4,5},{5,4},{6,7},{7,6},{8,9},{9,8},{10,11... | collective-permute-start | bytes 12582920 | tf_op jit(solution)/shard_map/ppermute | solution.py:139
  20.4 13.5 %all-to-all-start = ((bf16[32,4,8,256]{3,2,1,0:T(8,128)(2,1)}), bf16[32,4,8,256]{3,2,1,0:T(8,128)(2,1)S(1)}, u32[]{:S(2)}, u32[]{:S(2)}) async-start(bf16[32,4,8,256]{3,2,1,0:T(8,128)(2,1)} %bitcast.100), calls=%async_computation | async-start | bytes 1048576 | tf_op jit(solution)/shard_map/all_to_all | solution.py:140
  33.9 5.3 %slice_bitcast_fusion.8 = (bf16[2,2,2,128,256]{4,0,3,2,1:T(2,128)(2,1)}, bf16[2,2,2,256,128]{3,0,4,2,1:T(2,128)(2,1)}, bf16[2,2,2,256,128]{3,0,4,2,1:T(2,128)(2,...) fusion(bf16[8,2,2,128,2,256]{5,4,3,2,1,0:T(2,128)(2,1)} %param.5), kind=kLoop, calls=%fused_computation.8 | loop fusion | bytes 8388608 | tf_op jit(solution)/shard_map/transpose | solution.py:131
  39.3 0.5 copy.8
  40.3 1.4 copy.11
  41.7 1.9 %copy.5 = bf16[2,2,2,128,256]{4,3,2,1,0:T(8,128)(2,1)} copy(bf16[2,2,2,128,256]{4,0,3,2,1:T(2,128)(2,1)} %get-tuple-element.20) | data formatting | bytes 1048576 | tf_op jit(solution)/shard_map/transpose | solution.py:131
  43.6 2.0 %copy.6 = bf16[2,2,2,256,128]{4,3,2,1,0:T(8,128)(2,1)} copy(bf16[2,2,2,256,128]{3,0,4,2,1:T(2,128)(2,1)} %get-tuple-element.19) | data formatting | bytes 1048576 | tf_op jit(solution)/shard_map/transpose | solution.py:130
  45.7 5.5 %slice_bitcast_fusion = (bf16[2,2,2,128,256]{4,0,3,2,1:T(2,128)(2,1)}, bf16[2,2,2,256,128]{3,0,4,2,1:T(2,128)(2,1)}, bf16[2,2,2,256,128]{3,0,4,2,1:T(2,128)(2,1)...) fusion(bf16[8,2,2,128,2,256]{5,4,3,2,1,0:T(2,128)(2,1)} %collec, ...), kind=kLoop, calls=%fused_computation | loop fusion | bytes 8388608 | tf_op jit(solution)/shard_map/transpose | solution.py:131
  51.2 0.9 copy.12
  52.1 2.0 %copy.13 = bf16[2,2,2,256,128]{4,3,2,1,0:T(8,128)(2,1)} copy(bf16[2,2,2,256,128]{3,0,4,2,1:T(2,128)(2,1)} %get-tuple-element.11) | data formatting | bytes 1048576 | tf_op jit(solution)/shard_map/transpose | solution.py:130
  54.1 1.9 %copy.14 = bf16[2,2,2,128,256]{4,3,2,1,0:T(8,128)(2,1)} copy(bf16[2,2,2,128,256]{4,0,3,2,1:T(2,128)(2,1)} %get-tuple-element.10) | data formatting | bytes 1048576 | tf_op jit(solution)/shard_map/transpose | solution.py:131
  56.1 2.0 %copy.15 = bf16[2,2,2,256,128]{4,3,2,1,0:T(8,128)(2,1)} copy(bf16[2,2,2,256,128]{3,0,4,2,1:T(2,128)(2,1)} %get-tuple-element.9) | data formatting | bytes 1048576 | tf_op jit(solution)/shard_map/transpose | solution.py:130
  58.0 1.9 %copy.16 = bf16[2,2,2,128,256]{4,3,2,1,0:T(8,128)(2,1)} copy(bf16[2,2,2,128,256]{4,0,3,2,1:T(2,128)(2,1)} %get-tuple-element.8) | data formatting | bytes 1048576 | tf_op jit(solution)/shard_map/transpose | solution.py:131
  60.0 2.0 %copy.17 = bf16[2,2,2,256,128]{4,3,2,1,0:T(8,128)(2,1)} copy(bf16[2,2,2,256,128]{3,0,4,2,1:T(2,128)(2,1)} %get-tuple-element.7) | data formatting | bytes 1048576 | tf_op jit(solution)/shard_map/transpose | solution.py:130
  61.9 2.0 %copy.18 = bf16[2,2,2,256,128]{4,3,2,1,0:T(8,128)(2,1)} copy(bf16[2,2,2,256,128]{3,0,4,2,1:T(2,128)(2,1)} %get-tuple-element.6) | data formatting | bytes 1048576 | tf_op jit(solution)/shard_map/transpose | solution.py:130
  63.9 34.6 %all-to-all-done.got_ref = bf16[32,4,8,256]{3,2,1,0:T(8,128)(2,1)S(1)} async-done(((bf16[32,4,8,256]{3,2,1,0:T(8,128)(2,1)}), bf16[32,4,8,256]{3,2,1,0:T(8,128)(2,1)S(1)}, u32[]{:S(2)}, u32[]{:S(2)}) %all-to-all-start) | async-done | bytes 524320 | tf_op jit(solution)/shard_map/all_to_all | solution.py:140
  98.6 1.0 copy-done
  99.6 1.0 copy-done.1
  100.6 1.0 copy-done.2
  101.7 1.0 copy-done.4
  102.7 1.0 copy-done.5
  103.8 1.0 copy-done.6
  104.8 1.0 copy-done.7
  105.9 1.0 copy-done.8
  106.9 1.0 copy-done.9
  107.9 7.4 %chain.1 = bf16[32,4,8,256]{3,2,1,0:T(8,128)(2,1)S(1)} custom-call(f32[8,2,2,2]{3,2,1,0:T(2,128)S(1)} %copy.22.proj_ref, s32[1,8]{1,0:T(1,128)S(1)} %copy-done.10, bf16[32,4,8,256]{3,2,1,0:T(8,128)(2,1)S(1)} %all-to-all-done.got_ref, bf16[2,4,128,256]{3,2,1,0:T(8,128)(2,1)S(1)} %bitcast.91, bf16[2,4,256,128]{3,2,1,0:T(8,128)(2,1)S(1)} %bitcast.92, ...), custom_call_target="tpu_custom_call" | custom-call | flops 3758096384 | bytes 8388608 | tf_op jit(solution)/shard_map/chain/pallas_call | solution.py:146
  115.4 0.8 copy-done.3
  116.2 4.8 %all-to-all-start.1 = ((bf16[32,4,8,256]{3,2,1,0:T(8,128)(2,1)}), bf16[32,4,8,256]{3,2,1,0:T(8,128)(2,1)S(1)}, u32[]{:S(2)}, u32[]{:S(2)}) async-start(bf16[32,4,8,256]{3,2,1,0:T(8,128)(2,1)} %copy-done.3), calls=%async_computation.1 | async-start | bytes 1048576 | tf_op jit(solution)/shard_map/all_to_all | solution.py:161
  121.0 1.1 copy.20
  122.1 1.1 copy.21
  123.2 61.1 %all-to-all-done.1.got_ref = bf16[32,4,8,256]{3,2,1,0:T(8,128)(2,1)S(1)} async-done(((bf16[32,4,8,256]{3,2,1,0:T(8,128)(2,1)}), bf16[32,4,8,256]{3,2,1,0:T(8,128)(2,1)S(1)}, u32[]{:S(2)}, u32[]{:S(2)}) %all-to-all-start.1) | async-done | bytes 524320 | tf_op jit(solution)/shard_map/all_to_all | solution.py:161
  184.4 2.6 %last.1 = f32[32,2,2,8,256]{4,3,2,1,0:T(8,128)} custom-call(f32[8,2,2,2]{3,2,1,0:T(2,128)S(1)} %copy.22.proj_ref, s32[1,8]{1,0:T(1,128)S(1)} %copy-done.10, bf16[32,4,8,256]{3,2,1,0:T(8,128)(2,1)S(1)} %all-to-all-done.1.got_ref, bf16[2,4,128,256]{3,2,1,0:T(8,128)(2,1)S(1)} %bitcast.84, bf16[2,4,128,256]{3,2,1,0:T(8,128)(2,1)S(1)} %bitcast.85), custom_call_target="tpu_custom_call" | custom-call | flops 536870912 | bytes 3145728 | tf_op jit(solution)/shard_map/last/pallas_call | solution.py:162
  (19 shorter events, 0.7 us)
Async XLA Ops:
  0.0 45.7 %collective-permute-start = (bf16[8,2,2,128,2,256]{5,4,3,2,1,0:T(2,128)(2,1)}, bf16[8,2,2,128,2,256]{5,4,3,2,1,0:T(2,128)(2,1)}, u32[]{:S(2)}, u32[]{:S(2)}) collective-permute-start(bf16[8,2,2,128,2,256]{5,4,3,2,1,0:T(2,128)(2,1)} %param.5), channel_id=1, source_target_pairs={{0,1},{1,0},{2,3},{3,2},{4,5},{5,4},{6,7},{7,6},{8,9},{9,8},{10,11... | collective-permute-start | bytes 12582920 | tf_op jit(solution)/shard_map/ppermute | solution.py:139
  20.4 78.1 %all-to-all-start = ((bf16[32,4,8,256]{3,2,1,0:T(8,128)(2,1)}), bf16[32,4,8,256]{3,2,1,0:T(8,128)(2,1)S(1)}, u32[]{:S(2)}, u32[]{:S(2)}) async-start(bf16[32,4,8,256]{3,2,1,0:T(8,128)(2,1)} %bitcast.100), calls=%async_computation | async-start | bytes 1048576 | tf_op jit(solution)/shard_map/all_to_all | solution.py:140
  39.2 6.4 %copy-start.11 = (f32[8,2,2,2]{0,3,2,1:T(2,128)S(1)}, f32[8,2,2,2]{0,3,2,1:T(2,128)}, u32[]{:S(2)}) copy-start(f32[8,2,2,2]{0,3,2,1:T(2,128)} %param.6) | copy-start | bytes 772
  51.2 47.3 %copy-start.10 = (s32[1,8]{1,0:T(1,128)S(1)}, s32[1,8]{1,0:T(1,128)}, u32[]{:S(2)}) copy-start(s32[1,8]{1,0:T(1,128)} %bits_ref.3) | copy-start | bytes 100
  98.6 1.0 copy-start
  99.6 1.0 copy-start.1
  100.6 1.0 copy-start.2
  101.7 1.0 copy-start.4
  102.7 1.0 copy-start.5
  103.8 1.0 copy-start.6
  104.8 1.0 copy-start.7
  105.8 1.0 copy-start.8
  106.9 1.0 copy-start.9
  115.4 0.8 copy-start.3
  116.2 68.2 %all-to-all-start.1 = ((bf16[32,4,8,256]{3,2,1,0:T(8,128)(2,1)}), bf16[32,4,8,256]{3,2,1,0:T(8,128)(2,1)S(1)}, u32[]{:S(2)}, u32[]{:S(2)}) async-start(bf16[32,4,8,256]{3,2,1,0:T(8,128)(2,1)} %copy-done.3), calls=%async_computation.1 | async-start | bytes 1048576 | tf_op jit(solution)/shard_map/all_to_all | solution.py:161
